TPU v7x, 32 devices: a whole 2x2x4 slice. The times are simulated.
32 devices in a mesh: col: 4 (over z), row: 8 (over y, x, core).
Axes of the slice: x: 2, y: 2, z: 4, core: 2. Of those that a mesh axis runs over, the one named last changes fastest.
Arguments:
- vel_x: float32 [75, 2, 128, 768], P(None, None, 'row', 'col')
- vel_y: float32 [75, 2, 128, 768], P(None, None, 'row', 'col')
- pot_temp: float32 [75, 2, 128, 768], P(None, None, 'row', 'col')
- salinity: float32 [75, 2, 128, 768], P(None, None, 'row', 'col')
- surf_eta: float32 [2, 128, 768], P(None, 'row', 'col')
- trans_x: float32 [2, 128, 768], P(None, 'row', 'col')
- trans_y: float32 [2, 128, 768], P(None, 'row', 'col')
- col_depth: float32 [128, 768], P('row', 'col')
- wet_levels: int32 [128, 768], P('row', 'col')
- avg_weights: float32 [30], replicated
Outputs:
- output 1: float32 [2, 128, 768], P(None, 'row', 'col')
- output 2: float32 [2, 128, 768], P(None, 'row', 'col')
- output 3: float32 [2, 128, 768], P(None, 'row', 'col')
- output 4: float32 [75, 2, 128, 768], P(None, None, 'row', 'col')
- output 5: float32 [75, 2, 128, 768], P(None, None, 'row', 'col')
- output 6: float32 [75, 2, 128, 768], P(None, None, 'row', 'col')
- output 7: float32 [75, 2, 128, 768], P(None, None, 'row', 'col')
All inputs are finite; a program needn't handle non-finite values.
Results may differ from a plain program's by a relative error of at most 0.001.
Values sent between devices are 32-bit elements.
A program may use at most 1 GiB of HBM per device.

v0:
```python
import functools
import numpy as np
import jax
import jax.numpy as jnp
from jax import lax
from jax.experimental import pallas as pl
from jax.experimental.pallas import tpu as pltpu
from jax.sharding import PartitionSpec as P

WAVE_COURANT = 0.4
THERM_EXP = 0.2
HALINE_CON = 0.15
PRESS_SCALE = 0.5
VISC_NUMBER = 1.0
DIFF_NUMBER = 0.5
SUBCYCLES = 30
HALO = 32
ROWS, WIDTH, PADDED, LANES = 16, 192, 256, 128
MESH = pl.DeviceIdType.MESH
F32 = jnp.float32


def solve_tables(level_count):
    rows = []
    for strength in (VISC_NUMBER, DIFF_NUMBER):
        inner, last = np.zeros(level_count), np.zeros(level_count)
        inner[0], last[0] = 1.0 + strength, 1.0
        for k in range(1, level_count):
            inner[k] = 1.0 + 2.0 * strength - strength * strength / inner[k - 1]
            last[k] = 1.0 + strength - strength * strength / inner[k - 1]
        rows += [1.0 / inner, 1.0 / last, strength / inner]
    return np.concatenate(rows).astype(np.float32)


def level_chunk(level_count):
    for size in (15, 5, 4, 3, 2):
        if level_count % size == 0:
            return size
    return 1


def step_kernel(
    row_count, col_count, level_count,
    table, weights, kmt_in, depth_in, eta_in, tx_in, ty_in, u_hbm, v_hbm, t_hbm, s_hbm,
    pu, pv, pt, ps, corr, faces, avg,
    ub, vb, tb, sb, rows_n, rows_s, kmt_n, pack_w, pack_e, col_e, col_w, corner_se, corner_nw,
    edge_e, edge_w, wide, fedge_e, fedge_w, wide_f, coef,
    load_sem, row_send, row_recv, misc_send, misc_recv, wide_send, wide_recv,
):
    K = level_count
    size = level_chunk(K)
    chunks = K // size
    r = lax.axis_index("row")
    c = lax.axis_index("col")
    east = lax.rem(c + 1, col_count)
    west = lax.rem(c + col_count - 1, col_count)
    has_n, has_s = r < row_count - 1, r > 0
    has_nn, has_ss = r < row_count - 2, r > 1
    fields_hbm = (u_hbm, v_hbm, t_hbm, s_hbm)
    fields = (ub, vb, tb, sb)

    loads = [pltpu.make_async_copy(src, dst, load_sem.at[i]) for i, (src, dst) in enumerate(zip(fields_hbm, fields))]
    for copy in loads:
        copy.start()

    wide[...] = jnp.zeros_like(wide)
    wide_f[...] = jnp.zeros_like(wide_f)

    @pl.when(jnp.logical_not(has_n))
    def _():
        rows_n[...] = jnp.zeros_like(rows_n)
        kmt_n[...] = jnp.zeros_like(kmt_n)
        corner_nw[...] = jnp.zeros_like(corner_nw)

    @pl.when(jnp.logical_not(has_s))
    def _():
        rows_s[...] = jnp.zeros_like(rows_s)
        corner_se[...] = jnp.zeros_like(corner_se)

    barrier = pltpu.get_barrier_semaphore()

    def signal(**where):
        pl.semaphore_signal(barrier, inc=1, device_id=where, device_id_type=MESH)

    signal(col=east)
    signal(col=west)

    @pl.when(has_n)
    def _():
        signal(row=r + 1)
        signal(row=r + 1, col=west)

    @pl.when(has_s)
    def _():
        signal(row=r - 1)
        signal(row=r - 1, col=east)

    @pl.when(has_nn)
    def _():
        signal(row=r + 2)

    @pl.when(has_ss)
    def _():
        signal(row=r - 2)

    def one(flag):
        return flag.astype(jnp.int32)

    pl.semaphore_wait(barrier, 2 + 2 * one(has_n) + 2 * one(has_s) + one(has_nn) + one(has_ss))

    def remote(src, dst, ssem, rsem, **where):
        return pltpu.make_async_remote_copy(src_ref=src, dst_ref=dst, send_sem=ssem, recv_sem=rsem, device_id=where, device_id_type=MESH)

    kmt_copy = remote(kmt_in.at[0:1, :], kmt_n, misc_send.at[4], misc_recv.at[4], row=r - 1)

    def row_copy(side, i, f):
        levels = pl.ds(i * size, size)
        if side == 0:
            return remote(fields_hbm[f].at[levels, :, 0, :], rows_n.at[levels, 2 * f:2 * f + 2, :], row_send.at[0, i, f], row_recv.at[0, i, f], row=r - 1)
        return remote(fields_hbm[f].at[levels, :, 15, :], rows_s.at[levels, 2 * f:2 * f + 2, :], row_send.at[1, i, f], row_recv.at[1, i, f], row=r + 1)

    @pl.when(has_s)
    def _():
        kmt_copy.start()

    for i in range(chunks):
        @pl.when(has_s)
        def _():
            for f in range(4):
                row_copy(0, i, f).start()

        @pl.when(has_n)
        def _():
            for f in range(2):
                row_copy(1, i, f).start()

    @pl.when(has_n)
    def _():
        for i in range(chunks):
            for f in (2, 3):
                row_copy(1, i, f).start()

    lane = lax.broadcasted_iota(jnp.int32, (ROWS, LANES), 1)
    lane1 = lax.broadcasted_iota(jnp.int32, (1, LANES), 1)
    lane_all = lax.broadcasted_iota(jnp.int32, (ROWS, PADDED), 1)
    row_id = lax.broadcasted_iota(jnp.int32, (ROWS, PADDED), 0)

    def padded(x):
        return jnp.concatenate([x, jnp.zeros((x.shape[0], 64), x.dtype)], axis=1)

    kmt = padded(kmt_in[...]).astype(F32)
    own = pl.ds(HALO, ROWS)
    wide[0, own, :] = jnp.where(kmt > 0.5, padded(depth_in[...]), 0.0)
    for m in range(2):
        wide[1 + m, own, :] = padded(eta_in[m])
        wide[3 + m, own, :] = padded(tx_in[m])
        wide[5 + m, own, :] = padded(ty_in[m])

    edge_copies = [
        remote(wide.at[:, own, 0:LANES], edge_e, misc_send.at[5], misc_recv.at[5], col=west),
        remote(wide.at[:, own, LANES:PADDED], edge_w, misc_send.at[6], misc_recv.at[6], col=east),
    ]

    for copy in loads:
        copy.wait()
    for copy in edge_copies:
        copy.start()

    for f in range(4):
        def gather(k, acc):
            out = []
            for m in range(2):
                a = fields[f][k, m, :, 0:LANES]
                b = padded(fields[f][k, m, :, LANES:WIDTH])
                out.append(jnp.where(lane == k, pltpu.roll(a, k, 1), acc[2 * m]))
                out.append(jnp.where(lane == k, pltpu.roll(b, lax.rem(k + 65, LANES), 1), acc[2 * m + 1]))
            return tuple(out)

        zero = jnp.zeros((ROWS, LANES), F32)
        acc = lax.fori_loop(0, K, gather, (zero,) * 4, unroll=5)
        for m in range(2):
            pack_w[f, m] = acc[2 * m] if (f, m) != (0, 0) else jnp.where(lane == 127, pltpu.roll(kmt[:, 0:LANES], 127, 1), acc[0])
            pack_e[f, m] = acc[2 * m + 1]

    pack_copies = [
        remote(pack_w, col_e, misc_send.at[0], misc_recv.at[0], col=west),
        remote(pack_e, col_w, misc_send.at[1], misc_recv.at[1], col=east),
    ]
    for copy in pack_copies:
        copy.start()
    corner_v = remote(pack_w.at[1, :, 8:ROWS, :], corner_se, misc_send.at[2], misc_recv.at[2], row=r + 1, col=west)
    corner_u = remote(pack_e.at[0, :, 0:8, :], corner_nw, misc_send.at[3], misc_recv.at[3], row=r - 1, col=east)

    @pl.when(has_n)
    def _():
        corner_v.start()

    @pl.when(has_s)
    def _():
        corner_u.start()

    def with_edges(x, from_east, from_west):
        b = jnp.where(lane < 64, x[:, LANES:PADDED], jnp.where(lane < 96, pltpu.roll(from_east, 64, 1), pltpu.roll(from_west, 64, 1)))
        return jnp.concatenate([x[:, 0:LANES], b], axis=1)

    def spread(buf, first_sem):
        src = buf.at[:, own, :]
        return (
            (has_n, remote(src, buf.at[:, pl.ds(ROWS, ROWS), :], wide_send.at[first_sem], wide_recv.at[first_sem], row=r + 1)),
            (has_s, remote(src, buf.at[:, pl.ds(48, ROWS), :], wide_send.at[first_sem + 1], wide_recv.at[first_sem + 1], row=r - 1)),
            (has_nn, remote(src, buf.at[:, pl.ds(0, ROWS), :], wide_send.at[first_sem + 2], wide_recv.at[first_sem + 2], row=r + 2)),
            (has_ss, remote(src, buf.at[:, pl.ds(64, ROWS), :], wide_send.at[first_sem + 3], wide_recv.at[first_sem + 3], row=r - 2)),
        )

    def start_spread(copies):
        for there, copy in copies:
            @pl.when(there)
            def _():
                copy.start()

    def finish_spread(copies):
        arrives = (has_s, has_n, has_ss, has_nn)
        for (there, copy), here in zip(copies, arrives):
            @pl.when(there)
            def _():
                copy.wait_send()

            @pl.when(here)
            def _():
                copy.wait_recv()

    for copy in edge_copies:
        copy.wait()
    for p in range(7):
        wide[p, own, :] = with_edges(wide[p, own, :], edge_e[p], edge_w[p])
    static_copies = spread(wide, 0)
    start_spread(static_copies)

    for copy in pack_copies:
        copy.wait()

    @pl.when(has_n)
    def _():
        corner_v.wait_send()
        kmt_copy.wait_recv()
        corner_u.wait_recv()

    @pl.when(has_s)
    def _():
        corner_u.wait_send()
        kmt_copy.wait_send()
        corner_v.wait_recv()

    def roll_e(x):
        return pltpu.roll(x, 255, 1)

    def roll_w(x):
        return pltpu.roll(x, 1, 1)

    def from_north(x, edge):
        return jnp.where(row_id == 15, edge, pltpu.roll(x, 15, 0))

    def from_south(x, edge):
        return jnp.where(row_id == 0, edge, pltpu.roll(x, 1, 0))

    kmt_east = jnp.where(lane_all == 191, jnp.concatenate([lane.astype(F32), pltpu.roll(col_e[0, 0], 64, 1)], axis=1), roll_e(kmt))
    kmt_north = from_north(kmt, padded(kmt_n[...]).astype(F32))
    in_block = lane_all < WIDTH
    kmt_cell = jnp.where(in_block, kmt, 0.0)
    mu = jnp.where(in_block, jnp.minimum(kmt, kmt_east), 0.0)
    mv = jnp.where(in_block, jnp.minimum(kmt, kmt_north), 0.0)
    faces[0] = mu
    faces[1] = mv
    faces[2] = kmt_cell

    def extended(f, k, m):
        b = padded(fields[f][k, m, :, LANES:WIDTH])
        to_east = pltpu.roll(col_e[f, m], lax.rem(WIDTH - k, LANES), 1)
        to_west = pltpu.roll(col_w[f, m], lax.rem(255 - k, LANES), 1)
        b = jnp.where(lane < 64, b, jnp.where(lane == 64, to_east, to_west))
        return jnp.concatenate([fields[f][k, m, :, 0:LANES], b], axis=1)

    def edge_row(rows, f, k, m):
        return padded(rows[k, pl.ds(2 * f + m, 1), :])

    def solve_factor(depth, k, first):
        inner, last = table[first * K + k], table[(first + 1) * K + k]
        kf = k.astype(F32)
        return jnp.where(depth > kf + 1.0, inner, jnp.where(depth > kf, last, 0.0))

    scale = PRESS_SCALE / K

    def momentum(k, carry):
        out = []
        kf = k.astype(F32)
        for m in range(2):
            total, total_n, gu_sum, gv_sum, side_u, side_v = carry[m]
            u, v = extended(0, k, m), extended(1, k, m)
            t, s = extended(2, k, m), extended(3, k, m)
            density = HALINE_CON * s - THERM_EXP * t
            total = total + density
            pressure = scale * (total - 0.5 * density)
            density_n = HALINE_CON * edge_row(rows_n, 3, k, m) - THERM_EXP * edge_row(rows_n, 2, k, m)
            total_n = total_n + density_n
            pressure_n = scale * (total_n - 0.5 * density_n)
            un_edge = edge_row(rows_n, 0, k, m)
            nw = pltpu.roll(corner_nw[m], lax.rem(255 - k, LANES), 1)[0:1, :]
            un_edge = jnp.concatenate([un_edge[:, 0:LANES], jnp.where(lane1 == 127, nw, un_edge[:, LANES:PADDED])], axis=1)
            vs_edge = edge_row(rows_s, 1, k, m)
            se = pltpu.roll(corner_se[m], lax.rem(WIDTH - k, LANES), 1)[7:8, :]
            vs_edge = jnp.concatenate([vs_edge[:, 0:LANES], jnp.where(lane1 == 64, se, vs_edge[:, LANES:PADDED])], axis=1)
            u_n, u_s = from_north(u, un_edge), from_south(u, edge_row(rows_s, 0, k, m))
            v_n, v_s = from_north(v, edge_row(rows_n, 1, k, m)), from_south(v, vs_edge)
            p_n = from_north(pressure, pressure_n)
            v_pair = v + v_s
            u_pair = u + u_n
            vu = 0.125 * (v_pair + roll_e(v_pair))
            uv = 0.125 * (u_pair + roll_w(u_pair))
            gu = pressure - roll_e(pressure) - 0.5 * u * (roll_e(u) - roll_w(u)) - vu * (u_n - u_s)
            gv = pressure - p_n - uv * (roll_e(v) - roll_w(v)) - 0.5 * v * (v_n - v_s)
            gu = jnp.where(mu > kf, gu, 0.0)
            gv = jnp.where(mv > kf, gv, 0.0)
            side_u = (u + gu + VISC_NUMBER * side_u) * solve_factor(mu, k, 0)
            side_v = (v + gv + VISC_NUMBER * side_v) * solve_factor(mv, k, 0)
            pu[k, m] = side_u[:, 0:WIDTH]
            pv[k, m] = side_v[:, 0:WIDTH]
            out.append((total, total_n, gu_sum + gu, gv_sum + gv, side_u, side_v))
        return tuple(out)

    zero = jnp.zeros((ROWS, PADDED), F32)
    zero_row = jnp.zeros((1, PADDED), F32)
    carry = ((zero, zero_row, zero, zero, zero, zero),) * 2
    for i in range(chunks):
        @pl.when(has_n)
        def _():
            for f in range(4):
                row_copy(0, i, f).wait_recv()

        @pl.when(has_s)
        def _():
            for f in range(2):
                row_copy(1, i, f).wait_recv()

        carry = lax.fori_loop(i * size, (i + 1) * size, momentum, carry)

    count_u = jnp.maximum(mu, 1.0)
    count_v = jnp.maximum(mv, 1.0)
    for m in range(2):
        wide_f[m, own, :] = carry[m][2] / count_u
        wide_f[2 + m, own, :] = carry[m][3] / count_v
    force_edges = [
        remote(wide_f.at[:, own, 0:LANES], fedge_e, misc_send.at[7], misc_recv.at[7], col=west),
        remote(wide_f.at[:, own, LANES:PADDED], fedge_w, misc_send.at[8], misc_recv.at[8], col=east),
    ]
    for copy in force_edges:
        copy.start()

    @pl.when(has_s)
    def _():
        for i in range(chunks):
            for f in (2, 3):
                row_copy(1, i, f).wait_recv()

    def tracer(f, dest):
        def level(k, carry):
            out = []
            kf = k.astype(F32)
            factor = solve_factor(kmt_cell, k, 3)
            for m in range(2):
                u, v, t = extended(0, k, m), extended(1, k, m), extended(f, k, m)
                t_n = from_north(t, edge_row(rows_n, f, k, m))
                flux_x = 0.5 * u * (t + roll_e(t))
                flux_y = 0.5 * v * (t + t_n)
                flux_s = 0.5 * edge_row(rows_s, 1, k, m) * (edge_row(rows_s, f, k, m) + t[0:1, :])
                moved = t - (flux_x - roll_w(flux_x) + flux_y - from_south(flux_y, flux_s))
                side = (moved + DIFF_NUMBER * carry[m]) * factor
                dest[k, m] = side[:, 0:WIDTH]
                out.append(side)
            return tuple(out)

        last = lax.fori_loop(0, K, level, (zero, zero))

        def back(j, carry):
            k = K - 2 - j
            ratio = table[5 * K + k]
            out = []
            for m in range(2):
                x = dest[k, m] + ratio * carry[m]
                dest[k, m] = x
                out.append(x)
            return tuple(out)

        lax.fori_loop(0, K - 1, back, tuple(x[:, 0:WIDTH] for x in last))

    tracer(2, pt)

    for copy in force_edges:
        copy.wait()
    for p in range(4):
        wide_f[p, own, :] = with_edges(wide_f[p, own, :], fedge_e[p], fedge_w[p])
    force_copies = spread(wide_f, 4)
    start_spread(force_copies)

    tracer(3, ps)

    def back(j, carry):
        k = K - 2 - j
        ratio = table[2 * K + k]
        out = []
        for m in range(2):
            xu, xv, su, sv = carry[m]
            xu = pu[k, m] + ratio * xu
            xv = pv[k, m] + ratio * xv
            pu[k, m] = xu
            pv[k, m] = xv
            out.append((xu, xv, su + xu, sv + xv))
        return tuple(out)

    start = tuple(tuple(carry[m][i][:, 0:WIDTH] for i in (4, 5, 4, 5)) for m in range(2))
    ends = lax.fori_loop(0, K - 1, back, start)

    finish_spread(static_copies)
    finish_spread(force_copies)

    depth = wide[0]
    depth_e = pltpu.roll(depth, 255, 1)
    depth_n = pltpu.roll(depth, 79, 0)
    hu = jnp.where((depth > 0.0) & (depth_e > 0.0), 0.5 * (depth + depth_e), 0.0)
    hv = jnp.where((depth > 0.0) & (depth_n > 0.0), 0.5 * (depth + depth_n), 0.0)
    coef[0] = WAVE_COURANT * hu
    coef[1] = WAVE_COURANT * hv
    for m in range(2):
        wide_f[m] = hu * wide_f[m] * (1.0 / SUBCYCLES)
        wide_f[2 + m] = hv * wide_f[2 + m] * (1.0 / SUBCYCLES)
        for p in range(3):
            avg[2 * p + m] = zero

    def subcycle(n, _):
        weight = weights[n]
        for m in range(2):
            eta, tx, ty = wide[1 + m], wide[3 + m], wide[5 + m]
            eta = eta - WAVE_COURANT * (tx - pltpu.roll(tx, 1, 1) + ty - pltpu.roll(ty, 1, 0))
            tx = tx + wide_f[m] - coef[0] * (pltpu.roll(eta, 255, 1) - eta)
            ty = ty + wide_f[2 + m] - coef[1] * (pltpu.roll(eta, 79, 0) - eta)
            wide[1 + m] = eta
            wide[3 + m] = tx
            wide[5 + m] = ty
            mine = slice(HALO, HALO + ROWS)
            avg[m] = avg[m] + weight * eta[mine]
            avg[2 + m] = avg[2 + m] + weight * tx[mine]
            avg[4 + m] = avg[4 + m] + weight * ty[mine]
        return 0

    lax.fori_loop(0, SUBCYCLES, subcycle, 0)

    mine = slice(HALO, HALO + ROWS)
    for m in range(2):
        corr[m] = avg[2 + m] / jnp.where(mu > 0.5, hu[mine], 1.0) - padded(ends[m][2]) / count_u
        corr[2 + m] = avg[4 + m] / jnp.where(mv > 0.5, hv[mine], 1.0) - padded(ends[m][3]) / count_v

    @pl.when(has_s)
    def _():
        for i in range(chunks):
            for f in range(4):
                row_copy(0, i, f).wait_send()

    @pl.when(has_n)
    def _():
        for i in range(chunks):
            for f in range(4):
                row_copy(1, i, f).wait_send()


def finish_kernel(size, pu, pv, pt, ps, corr, faces, avg, eta_o, tx_o, ty_o, u_o, v_o, t_o, s_o, sems):
    first = pl.program_id(0) * size
    through = [pltpu.make_async_copy(src, dst, sems.at[i]) for i, (src, dst) in enumerate(((pt, t_o), (ps, s_o)))]

    @pl.when(first == 0)
    def _():
        for copy in through:
            copy.start()
        for m in range(2):
            eta_o[m] = avg[m][:, 0:WIDTH]
            tx_o[m] = avg[2 + m][:, 0:WIDTH]
            ty_o[m] = avg[4 + m][:, 0:WIDTH]

    for j in range(size):
        level = (first + j).astype(F32)
        for m in range(2):
            for face, (src, dst) in enumerate(((pu, u_o), (pv, v_o))):
                wet = faces[face][:, 0:WIDTH] > level
                dst[j, m] = jnp.where(wet, src[first + j, m] + corr[2 * face + m][:, 0:WIDTH], 0.0)

    @pl.when(pl.program_id(0) == pl.num_programs(0) - 1)
    def _():
        for copy in through:
            copy.wait()


def solution(mesh):
    col_count, row_count = mesh.shape["col"], mesh.shape["row"]

    def local_step(vel_x, vel_y, pot_temp, salinity, surf_eta, trans_x, trans_y, col_depth, wet_levels, avg_weights):
        K = vel_x.shape[0]
        size = level_chunk(K)
        chunks = K // size
        table = jnp.asarray(solve_tables(K))
        smem = pl.BlockSpec(memory_space=pltpu.SMEM)
        vmem = pl.BlockSpec(memory_space=pltpu.VMEM)
        hbm = pl.BlockSpec(memory_space=pl.ANY)
        full = jax.ShapeDtypeStruct((K, 2, ROWS, WIDTH), F32)
        held = pltpu.VMEM((K, 2, ROWS, WIDTH), F32)
        dma = pltpu.SemaphoreType.DMA
        outs = pl.pallas_call(
            functools.partial(step_kernel, row_count, col_count, K),
            out_shape=(held,) * 4 + tuple(pltpu.VMEM((n, ROWS, PADDED), F32) for n in (4, 3, 6)),
            in_specs=[smem, smem] + [vmem] * 5 + [hbm] * 4,
            out_specs=(vmem,) * 7,
            scratch_shapes=[
                *[pltpu.VMEM((K, 2, ROWS, WIDTH), F32)] * 4,
                *[pltpu.VMEM((K, 8, WIDTH), F32)] * 2,
                pltpu.VMEM((1, WIDTH), jnp.int32),
                *[pltpu.VMEM((4, 2, ROWS, LANES), F32)] * 4,
                *[pltpu.VMEM((2, 8, LANES), F32)] * 2,
                *[pltpu.VMEM((7, ROWS, LANES), F32)] * 2,
                pltpu.VMEM((7, 80, PADDED), F32),
                *[pltpu.VMEM((4, ROWS, LANES), F32)] * 2,
                pltpu.VMEM((4, 80, PADDED), F32),
                pltpu.VMEM((2, 80, PADDED), F32),
                dma((4,)), dma((2, chunks, 4)), dma((2, chunks, 4)), dma((9,)), dma((9,)), dma((8,)), dma((8,)),
            ],
            compiler_params=pltpu.CompilerParams(collective_id=0, has_side_effects=True, vmem_limit_bytes=53 << 20),
            name="ocean_step",
        )(table, avg_weights, wet_levels, col_depth, surf_eta, trans_x, trans_y, vel_x, vel_y, pot_temp, salinity)

        small = jax.ShapeDtypeStruct((2, ROWS, WIDTH), F32)
        deep_out = pl.BlockSpec((size, 2, ROWS, WIDTH), lambda i: (i, 0, 0, 0))
        small_out = pl.BlockSpec((2, ROWS, WIDTH), lambda i: (0, 0, 0))
        return pl.pallas_call(
            functools.partial(finish_kernel, size),
            grid=(chunks,),
            out_shape=(small,) * 3 + (full,) * 4,
            in_specs=[vmem] * 7,
            out_specs=(small_out,) * 3 + (deep_out,) * 2 + (hbm,) * 2,
            scratch_shapes=[dma((2,))],
            compiler_params=pltpu.CompilerParams(vmem_limit_bytes=20 << 20),
            name="ocean_finish",
        )(*outs)

    spec_3d = P(None, None, "row", "col")
    spec_2d = P(None, "row", "col")
    spec_map = P("row", "col")
    return jax.shard_map(local_step, mesh=mesh, in_specs=(spec_3d,) * 4 + (spec_2d,) * 3 + (spec_map,) * 2 + (P(),), out_specs=(spec_2d,) * 3 + (spec_3d,) * 4, check_vma=False)
```

profile of v0, /device:TPU:1, one launch (start us, length us, event | category | flops | bytes accessed | tf_op | source)
XLA Modules:
  0.0 86.9 jit_solution(17211285560958024469)
XLA Ops:
  0.6 81.6 %ocean_step.1 = (f32[75,2,16,192]{3,2,1,0:T(8,128)S(1)}, f32[75,2,16,192]{3,2,1,0:T(8,128)S(1)}, f32[75,2,16,192]{3,2,1,0:T(8,128)S(1)}, f32[75,2,16,192]{3,2,1,...) custom-call(f32[450]{0:T(512)} %constant.2.clone.table, ...), custom_call_target="tpu_custom_call" | custom-call | tf_op jit(solution)/shard_map/ocean_step/pallas_call | solution.py:514
  82.3 4.7 %ocean_finish.1 = (f32[2,16,192]{2,1,0:T(8,128)}, f32[2,16,192]{2,1,0:T(8,128)}, f32[2,16,192]{2,1,0:T(8,128)}, f32[75,2,16,192]{3,2,1,0:T(8,128)}, f32[75,2,16,...) custom-call(f32[75,2,16,192]{3,2,1,0:T(8,128)S(1)} %get-tuple-element.14.pu, ...), custom_call_target="tpu_custom_call" | custom-call | tf_op jit(solution)/shard_map/ocean_finish/pallas_call | solution.py:539
where the time goes:
time: 87.1 us; the launch traced here: 86.9 us
  Pallas kernels  86.3 us (99%)
    pallas_call x1, Pallas kernels, local_step(): pl.pallas_call(functools.partial(step_kernel, row_count, col_count, K), o...  81.6 us
    pallas_call x1, Pallas kernels, local_step(): pl.pallas_call(functools.partial(finish_kernel, size), grid=(chunks,), ou...  4.67 us

commit v1 on v0

--- a/solution.py
+++ b/solution.py
@@ -43,13 +43,15 @@
     row_count, col_count, level_count,
     table, weights, kmt_in, depth_in, eta_in, tx_in, ty_in, u_hbm, v_hbm, t_hbm, s_hbm,
     pu, pv, pt, ps, corr, faces, avg,
-    ub, vb, tb, sb, rows_n, rows_s, kmt_n, pack_w, pack_e, col_e, col_w, corner_se, corner_nw,
+    ub, vb, tb, sb, rows_n, rows_s, send_n, send_s, kmt_n, pack_w, pack_e, col_e, col_w, corner_se, corner_nw,
     edge_e, edge_w, wide, fedge_e, fedge_w, wide_f, coef,
     load_sem, row_send, row_recv, misc_send, misc_recv, wide_send, wide_recv,
 ):
     K = level_count
     size = level_chunk(K)
     chunks = K // size
+    half = (size + 1) // 2
+    tile_count = size + half
     r = lax.axis_index("row")
     c = lax.axis_index("col")
     east = lax.rem(c + 1, col_count)
@@ -59,9 +61,13 @@
     fields_hbm = (u_hbm, v_hbm, t_hbm, s_hbm)
     fields = (ub, vb, tb, sb)
 
-    loads = [pltpu.make_async_copy(src, dst, load_sem.at[i]) for i, (src, dst) in enumerate(zip(fields_hbm, fields))]
-    for copy in loads:
-        copy.start()
+    loads = [
+        [pltpu.make_async_copy(src.at[pl.ds(i * size, size)], dst.at[pl.ds(i * size, size)], load_sem.at[i, f]) for f, (src, dst) in enumerate(zip(fields_hbm, fields))]
+        for i in range(chunks)
+    ]
+    for group in loads:
+        for copy in group:
+            copy.start()
 
     wide[...] = jnp.zeros_like(wide)
     wide_f[...] = jnp.zeros_like(wide_f)
@@ -113,32 +119,15 @@
 
     kmt_copy = remote(kmt_in.at[0:1, :], kmt_n, misc_send.at[4], misc_recv.at[4], row=r - 1)
 
-    def row_copy(side, i, f):
-        levels = pl.ds(i * size, size)
+    @pl.when(has_s)
+    def _():
+        kmt_copy.start()
+
+    def row_copy(side, i):
+        tiles = pl.ds(i * tile_count, tile_count)
         if side == 0:
-            return remote(fields_hbm[f].at[levels, :, 0, :], rows_n.at[levels, 2 * f:2 * f + 2, :], row_send.at[0, i, f], row_recv.at[0, i, f], row=r - 1)
-        return remote(fields_hbm[f].at[levels, :, 15, :], rows_s.at[levels, 2 * f:2 * f + 2, :], row_send.at[1, i, f], row_recv.at[1, i, f], row=r + 1)
-
-    @pl.when(has_s)
-    def _():
-        kmt_copy.start()
-
-    for i in range(chunks):
-        @pl.when(has_s)
-        def _():
-            for f in range(4):
-                row_copy(0, i, f).start()
-
-        @pl.when(has_n)
-        def _():
-            for f in range(2):
-                row_copy(1, i, f).start()
-
-    @pl.when(has_n)
-    def _():
-        for i in range(chunks):
-            for f in (2, 3):
-                row_copy(1, i, f).start()
+            return remote(send_s.at[tiles], rows_n.at[tiles], row_send.at[0, i], row_recv.at[0, i], row=r - 1)
+        return remote(send_n.at[tiles], rows_s.at[tiles], row_send.at[1, i], row_recv.at[1, i], row=r + 1)
 
     lane = lax.broadcasted_iota(jnp.int32, (ROWS, LANES), 1)
     lane1 = lax.broadcasted_iota(jnp.int32, (1, LANES), 1)
@@ -161,26 +150,56 @@
         remote(wide.at[:, own, LANES:PADDED], edge_w, misc_send.at[6], misc_recv.at[6], col=east),
     ]
 
-    for copy in loads:
-        copy.wait()
     for copy in edge_copies:
         copy.start()
 
+    sub = lax.broadcasted_iota(jnp.int32, (8, LANES), 0)
+
+    def pack_level(k, acc):
+        out, tiles = [], [[None, None], [None, None]]
+        for f in range(4):
+            for m in range(2):
+                halves = (fields[f][k, m, :, 0:LANES], padded(fields[f][k, m, :, LANES:WIDTH]))
+                for h in range(2):
+                    turned = pltpu.roll(halves[h], k if h == 0 else lax.rem(k + 65, LANES), 1)
+                    out.append(jnp.where(lane == k, turned, acc[len(out)]))
+                    for side in range(2):
+                        spot = 2 * f + m
+                        row = pltpu.roll(halves[h][8 * side:8 * side + 8], spot if side == 0 else (spot + 1) % 8, 0)
+                        old = tiles[side][h]
+                        tiles[side][h] = row if old is None else jnp.where(sub == spot, row, old)
+        return tuple(out), tiles
+
+    acc = (jnp.zeros((ROWS, LANES), F32),) * 16
+    lower = lax.broadcasted_iota(jnp.int32, (8, LANES), 1) < 64
+    for i in range(chunks):
+        def pack_pair(j, acc):
+            j2 = jnp.minimum(j + half, size - 1)
+            acc, one_level = pack_level(i * size + j, acc)
+            acc, other = pack_level(i * size + j2, acc)
+            for side, dest in enumerate((send_s, send_n)):
+                dest[i * tile_count + j] = one_level[side][0]
+                dest[i * tile_count + j2] = other[side][0]
+                dest[i * tile_count + size + j] = jnp.where(lower, one_level[side][1], pltpu.roll(other[side][1], 64, 1))
+            return acc
+
+        for copy in loads[i]:
+            copy.wait()
+        acc = lax.fori_loop(0, half, pack_pair, acc, unroll=2)
+
+        @pl.when(has_s)
+        def _():
+            row_copy(0, i).start()
+
+        @pl.when(has_n)
+        def _():
+            row_copy(1, i).start()
+
     for f in range(4):
-        def gather(k, acc):
-            out = []
-            for m in range(2):
-                a = fields[f][k, m, :, 0:LANES]
-                b = padded(fields[f][k, m, :, LANES:WIDTH])
-                out.append(jnp.where(lane == k, pltpu.roll(a, k, 1), acc[2 * m]))
-                out.append(jnp.where(lane == k, pltpu.roll(b, lax.rem(k + 65, LANES), 1), acc[2 * m + 1]))
-            return tuple(out)
-
-        zero = jnp.zeros((ROWS, LANES), F32)
-        acc = lax.fori_loop(0, K, gather, (zero,) * 4, unroll=5)
         for m in range(2):
-            pack_w[f, m] = acc[2 * m] if (f, m) != (0, 0) else jnp.where(lane == 127, pltpu.roll(kmt[:, 0:LANES], 127, 1), acc[0])
-            pack_e[f, m] = acc[2 * m + 1]
+            west_edge = acc[4 * f + 2 * m]
+            pack_w[f, m] = west_edge if f + m > 0 else jnp.where(lane == 127, pltpu.roll(kmt[:, 0:LANES], 127, 1), west_edge)
+            pack_e[f, m] = acc[4 * f + 2 * m + 1]
 
     pack_copies = [
         remote(pack_w, col_e, misc_send.at[0], misc_recv.at[0], col=west),
@@ -281,7 +300,11 @@
         return jnp.concatenate([fields[f][k, m, :, 0:LANES], b], axis=1)
 
     def edge_row(rows, f, k, m):
-        return padded(rows[k, pl.ds(2 * f + m, 1), :])
+        chunk = lax.div(k, size)
+        j = k - chunk * size
+        first, spot = chunk * tile_count, 2 * f + m
+        tail = pltpu.roll(rows[first + size + lax.rem(j, half)], 64 * one(j >= half), 1)
+        return jnp.concatenate([rows[first + j][spot:spot + 1], tail[spot:spot + 1]], axis=1)
 
     def solve_factor(depth, k, first):
         inner, last = table[first * K + k], table[(first + 1) * K + k]
@@ -333,13 +356,11 @@
     for i in range(chunks):
         @pl.when(has_n)
         def _():
-            for f in range(4):
-                row_copy(0, i, f).wait_recv()
+            row_copy(0, i).wait_recv()
 
         @pl.when(has_s)
         def _():
-            for f in range(2):
-                row_copy(1, i, f).wait_recv()
+            row_copy(1, i).wait_recv()
 
         carry = lax.fori_loop(i * size, (i + 1) * size, momentum, carry)
 
@@ -354,12 +375,6 @@
     ]
     for copy in force_edges:
         copy.start()
-
-    @pl.when(has_s)
-    def _():
-        for i in range(chunks):
-            for f in (2, 3):
-                row_copy(1, i, f).wait_recv()
 
     def tracer(f, dest):
         def level(k, carry):
@@ -461,14 +476,12 @@
     @pl.when(has_s)
     def _():
         for i in range(chunks):
-            for f in range(4):
-                row_copy(0, i, f).wait_send()
+            row_copy(0, i).wait_send()
 
     @pl.when(has_n)
     def _():
         for i in range(chunks):
-            for f in range(4):
-                row_copy(1, i, f).wait_send()
+            row_copy(1, i).wait_send()
 
 
 def finish_kernel(size, pu, pv, pt, ps, corr, faces, avg, eta_o, tx_o, ty_o, u_o, v_o, t_o, s_o, sems):
@@ -518,7 +531,7 @@
             out_specs=(vmem,) * 7,
             scratch_shapes=[
                 *[pltpu.VMEM((K, 2, ROWS, WIDTH), F32)] * 4,
-                *[pltpu.VMEM((K, 8, WIDTH), F32)] * 2,
+                *[pltpu.VMEM((chunks * (size + (size + 1) // 2), 8, LANES), F32)] * 4,
                 pltpu.VMEM((1, WIDTH), jnp.int32),
                 *[pltpu.VMEM((4, 2, ROWS, LANES), F32)] * 4,
                 *[pltpu.VMEM((2, 8, LANES), F32)] * 2,
@@ -527,7 +540,7 @@
                 *[pltpu.VMEM((4, ROWS, LANES), F32)] * 2,
                 pltpu.VMEM((4, 80, PADDED), F32),
                 pltpu.VMEM((2, 80, PADDED), F32),
-                dma((4,)), dma((2, chunks, 4)), dma((2, chunks, 4)), dma((9,)), dma((9,)), dma((8,)), dma((8,)),
+                dma((chunks, 4)), dma((2, chunks)), dma((2, chunks)), dma((9,)), dma((9,)), dma((8,)), dma((8,)),
             ],
             compiler_params=pltpu.CompilerParams(collective_id=0, has_side_effects=True, vmem_limit_bytes=53 << 20),
             name="ocean_step",

time: 87.1 us -> 82.7 us (0.949)
  Pallas kernels: 86.3 us -> 81.8 us
    pallas_call x1, Pallas kernels: 81.6 us -> 77.2 us  [local_step(): pl.pallas_call(functools.partial(step_kernel, row_count, col_count, K), o...]
where the time goes in v1:
time: 82.7 us; the launch traced here: 82.5 us
  Pallas kernels  81.8 us (99%)
    pallas_call x1, Pallas kernels, local_step(): pl.pallas_call(functools.partial(step_kernel, row_count, col_count, K), o...  77.2 us
    pallas_call x1, Pallas kernels, local_step(): pl.pallas_call(functools.partial(finish_kernel, size), grid=(chunks,), ou...  4.67 us

profile of v1, /device:TPU:1, one launch (start us, length us, event | category | flops | bytes accessed | tf_op | source)
XLA Modules:
  0.0 82.5 jit_solution(14365626767634610862)
XLA Ops:
  0.6 77.2 %ocean_step.1 = (f32[75,2,16,192]{3,2,1,0:T(8,128)S(1)}, f32[75,2,16,192]{3,2,1,0:T(8,128)S(1)}, f32[75,2,16,192]{3,2,1,0:T(8,128)S(1)}, f32[75,2,16,192]{3,2,1,...) custom-call(f32[450]{0:T(512)} %constant.2.clone.table, ...), custom_call_target="tpu_custom_call" | custom-call | tf_op jit(solution)/shard_map/ocean_step/pallas_call | solution.py:527
  77.8 4.7 %ocean_finish.1 = (f32[2,16,192]{2,1,0:T(8,128)}, f32[2,16,192]{2,1,0:T(8,128)}, f32[2,16,192]{2,1,0:T(8,128)}, f32[75,2,16,192]{3,2,1,0:T(8,128)}, f32[75,2,16,...) custom-call(f32[75,2,16,192]{3,2,1,0:T(8,128)S(1)} %get-tuple-element.14.pu, ...), custom_call_target="tpu_custom_call" | custom-call | tf_op jit(solution)/shard_map/ocean_finish/pallas_call | solution.py:552
